TPU v7x, 32 devices: a whole 2x2x4 slice. The times are simulated.
32 devices in a mesh: cells: 8 (over y, x, core), wells: 4 (over z).
Axes of the slice: x: 2, y: 2, z: 4, core: 2. Of those that a mesh axis runs over, the one named last changes fastest.
Arguments:
- cell_state: float32 [3, 4, 131072], P(None, 'wells', 'cells'), may hold values from -6 to 6
- cell_residual: float32 [3, 4, 131072], P(None, 'wells', 'cells'), may hold values from -6 to 6
- cell_block: float32 [9, 4, 131072], P(None, 'wells', 'cells'), may hold values from -4 to 4
- block_inverse: float32 [9, 4, 131072], P(None, 'wells', 'cells'), may hold values from -3.5 to 3.5
- perf_cells: int32 [4, 32, 128], P('wells'), may hold values from 0 to 131071, as said below
- perf_count: int32 [4, 32], P('wells'), may hold values from 32 to 128
- perf_index: float32 [4, 32, 128], P('wells'), may hold values from 0.2 to 2
- seg_parent: int32 [4, 32, 32], P('wells'), may hold values from 0 to 30, as said below
- seg_cond: float32 [4, 32, 32], P('wells'), may hold values from 0.5 to 4
- seg_state: float32 [3, 4, 32, 32], P(None, 'wells'), may hold values from -6 to 6
- seg_source: float32 [3, 4, 32, 32], P(None, 'wells'), may hold values from -6 to 6
Outputs:
- cell_update: float32 [3, 4, 131072], P(None, 'wells', 'cells')
- well_update: float32 [3, 4, 32, 32], P(None, 'wells', 'cells')
- residual_max: float32 [6], replicated
Inputs may be any that keep to these rules, and one draw needn't show every extreme that they name: seg_parent[..., 0] is 0; for s >= 1, seg_parent[..., s] lies between s - 3 and s - 1, so the segments of a well form a tree rooted at segment 0. `perf_cells`: in each region, take the wells in groups of 4 consecutive wells and the cells in blocks of 16384 consecutive cells; exactly 64 slots of each group, live or not, name a cell of each block.
All inputs are finite; a program needn't handle non-finite values.
Results may differ from a plain program's by a relative error of at most 0.0001.
Values sent between devices are 32-bit elements; how exact they have to be, the bound alone decides.
A program may use at most 128 MiB of HBM per device.

v0:
```python
import jax
import jax.numpy as jnp
from jax import lax
from jax.sharding import PartitionSpec as P


def expand_segments(values, slots):
    repeat = slots // values.shape[-1]
    wide = jnp.broadcast_to(values[..., None], values.shape + (repeat,))
    return wide.reshape(values.shape[:-1] + (slots,))


def segment_sums(values, segs):
    return jnp.sum(values.reshape(values.shape[:-1] + (segs, values.shape[-1] // segs)), axis=-1)


def perf_terms(jac_at, state_at, weight, seg_values):
    slots = weight.shape[-1]
    blocks = jac_at.reshape((3, 3) + weight.shape)
    kmat = jnp.sum(blocks[:, None] * blocks[None, :], axis=2)
    kmat = (kmat + jnp.eye(3, dtype=jnp.float32)[:, :, None, None]) * weight[None, None]
    differ = state_at - expand_segments(seg_values, slots)
    flow = jnp.sum(kmat * differ[None], axis=1)
    return (kmat, flow)


def solve_wells(ksum, rsum, parent, cond):
    segs = parent.shape[-1]
    count = parent.shape[0]
    index = jnp.arange(segs, dtype=jnp.int32)
    link = (parent[:, :, None] == index[None, None, :]) & (index[None, :, None] >= 1)
    adjacent = jnp.where(link, cond[:, :, None], jnp.float32(0.0))
    symmetric = adjacent + jnp.swapaxes(adjacent, 1, 2)
    eye_seg = jnp.eye(segs, dtype=jnp.float32)
    matrix = jnp.sum(symmetric, axis=2)[:, :, None] * eye_seg[None] - symmetric + eye_seg[None]
    eye_comp = jnp.eye(3, dtype=jnp.float32)
    blocks = jnp.transpose(ksum, (2, 3, 0, 1))
    dense = (
        matrix[:, :, None, :, None] * eye_comp[None, None, :, None, :]
        + blocks[:, :, :, None, :] * eye_seg[None, :, None, :, None]
    )
    dense = dense.reshape(count, 3 * segs, 3 * segs)
    rhs = jnp.transpose(rsum, (1, 2, 0)).reshape(count, 3 * segs)
    lower = jnp.linalg.cholesky(dense)

    def one_well(low, vec):
        return jax.scipy.linalg.cho_solve((low, True), vec)

    solved = jax.vmap(one_well)(lower, rhs)
    return jnp.transpose(solved.reshape(count, segs, 3), (2, 0, 1))


def on_device(
    cell_state,
    cell_residual,
    cell_block,
    block_inverse,
    perf_cells,
    perf_count,
    perf_index,
    seg_parent,
    seg_cond,
    seg_state,
    seg_source,
):
    shard_cells = cell_state.shape[2]
    region_wells = perf_cells.shape[1]
    slots = perf_cells.shape[2]
    segs = seg_parent.shape[2]
    ncells = lax.axis_size("cells")
    me = lax.axis_index("cells")
    owned = region_wells // ncells
    first = me * owned
    state = cell_state[:, 0]
    resid = cell_residual[:, 0]
    start = me * shard_cells
    offset = perf_cells[0] - start
    inside = (offset >= 0) & (offset < shard_cells)
    safe = jnp.clip(offset, 0, shard_cells - 1)
    live = jnp.arange(slots, dtype=jnp.int32)[None, :] < perf_count[0][:, None]
    weight = jnp.where(inside & live, perf_index[0], jnp.float32(0.0))
    jac_at = cell_block[:, 0][:, safe]
    state_at = state[:, safe]
    kmat, flow = perf_terms(jac_at, state_at, weight, seg_state[:, 0])
    table = jnp.concatenate([kmat.reshape(9, region_wells, slots), flow], axis=0)
    table = segment_sums(table, segs)
    summed = lax.psum_scatter(table, "cells", scatter_dimension=1, tiled=True)
    parent = lax.dynamic_slice_in_dim(seg_parent[0], first, owned, 0)
    cond = lax.dynamic_slice_in_dim(seg_cond[0], first, owned, 0)
    source = lax.dynamic_slice_in_dim(seg_source[:, 0], first, owned, 1)
    wells_here = summed.shape[1]
    ksum = summed[:9].reshape(3, 3, wells_here, segs)
    rsum = summed[9:] + source
    solved = solve_wells(ksum, rsum, parent, cond)
    well_max = jnp.max(jnp.abs(rsum), axis=(1, 2))
    every_well = lax.all_gather(solved, "cells", axis=1, tiled=True)
    spread = expand_segments(every_well, slots)
    delta = jnp.sum(kmat * spread[None], axis=1)
    correction = (
        jnp.zeros((3, shard_cells), jnp.float32).at[:, safe.reshape(-1)].add(delta.reshape(3, -1))
    )
    corrected = resid - correction
    cell_max = jnp.max(jnp.abs(corrected), axis=1)
    cell_top, well_top = lax.pmax((cell_max, well_max), ("cells", "wells"))
    scale = 1.0 / jnp.maximum(jnp.float32(1.0), cell_top)
    inverse = block_inverse[:, 0].reshape(3, 3, shard_cells)
    step = jnp.sum(inverse * corrected[None], axis=1) * scale[:, None]
    residual_max = jnp.concatenate([cell_top, well_top])
    return (step[:, None], solved[:, None], residual_max)


def solution(mesh):
    in_specs = (
        P(None, "wells", "cells"),
        P(None, "wells", "cells"),
        P(None, "wells", "cells"),
        P(None, "wells", "cells"),
        P("wells", None, None),
        P("wells", None),
        P("wells", None, None),
        P("wells", None, None),
        P("wells", None, None),
        P(None, "wells", None, None),
        P(None, "wells", None, None),
    )
    out_specs = (P(None, "wells", "cells"), P(None, "wells", "cells", None), P())
    return jax.shard_map(
        on_device, mesh=mesh, in_specs=in_specs, out_specs=out_specs, check_vma=False
    )
```

profile of v0, /device:TPU:0, one launch (start us, length us, event | category | flops | bytes accessed | tf_op | source)
XLA Modules:
  0.0 272.6 jit_solution(10672945761370054616)
XLA Ops:
  0.7 0.8 fusion.23
  1.5 6.1 %copy.131 = f32[9,1,16384]{0,2,1:T(8,128)} copy(f32[9,1,16384]{2,1,0:T(1,128)} %param.13) | data formatting | bytes 1179648 | tf_op args[2]
  7.5 14.2 %gather_fusion = f32[4096,9]{1,0:T(8,128)S(1)} fusion(f32[9,16384]{0,1:T(8,128)} %bitcast.90, s32[4096]{0:T(1024)S(1)} %get-tuple-element.27), kind=kCustom, calls=%fused_computation | custom fusion | bytes 311296 | tf_op jit(solution)/shard_map/gather | solution.py:82
  21.7 0.6 copy.132
  22.5 4.6 %copy.138 = f32[3,1,16384]{0,2,1:T(8,128)} copy(f32[3,1,16384]{2,1,0:T(1,128)S(1)} %copy-done.3) | data formatting | bytes 393216 | tf_op args[0]
  27.1 17.5 %gather_fusion.1 = f32[4096,3]{1,0:T(8,128)} fusion(f32[3,16384]{0,1:T(8,128)} %bitcast.91, s32[4096]{0:T(1024)S(1)} %get-tuple-element.27), kind=kCustom, calls=%fused_computation.1 | custom fusion | bytes 114688 | tf_op jit(solution)/shard_map/gather | solution.py:83
  44.6 0.3 copy.139
  44.9 0.4 broadcast_in_dim.76
  45.2 1.9 sub.50
  47.2 0.6 copy.140
  47.9 0.1 copy.141
  48.0 0.2 copy.135
  48.3 0.1 copy.136
  48.7 0.2 add_multiply_fusion
  48.9 0.6 maximum_reduce_fusion
  49.6 27.8 %all-reduce = f32[12,32,32]{2,1,0:T(8,128)S(1)} all-reduce(f32[12,32,32]{2,1,0:T(8,128)S(1)} %copy.142), channel_id=2, replica_groups=mesh['cells'=8,'wells'=4] {'cells'}, use_global_device_ids=true, to_apply=%region_4.5.clone | all-reduce | flops 12288 | bytes 98304
  77.4 0.6 dynamic-slice.3
  78.7 0.2 copy.143
  78.9 3.1 %mul.160 = f32[4,32,3,32,3]{4,3,2,1,0:T(8,128)} broadcast(f32[4,32,3,3]{3,2,1,0:T(4,128)S(1)} %copy.143), dimensions={0,1,2,4} | broadcast | bytes 152064 | tf_op jit(solution)/shard_map/mul | solution.py:40
  81.9 6.5 %mul.161 = f32[4,96,96]{2,1,0:T(8,128)S(1)} reshape(f32[4,32,3,32,3]{4,3,2,1,0:T(8,128)} %mul.160) | data formatting | bytes 294912 | tf_op jit(solution)/shard_map/mul | solution.py:40
  88.6 0.7 dynamic-slice_bitcast_fusion.1
  89.3 0.6 fusion.5
  89.9 3.5 %mul.150 = f32[4,32,3,32,3]{4,3,2,1,0:T(8,128)} broadcast(f32[4,32,32]{2,1,0:T(8,128)S(1)} %fusion.5), dimensions={0,1,3} | broadcast | bytes 163840 | tf_op jit(solution)/shard_map/mul | solution.py:39
  93.5 6.5 %mul.151 = f32[4,96,96]{2,1,0:T(8,128)S(1)} reshape(f32[4,32,3,32,3]{4,3,2,1,0:T(8,128)} %mul.150) | data formatting | bytes 294912 | tf_op jit(solution)/shard_map/mul | solution.py:39
  100.1 0.2 mul.152
  100.3 1.1 mul.153
  101.5 0.3 mul.162
  101.7 1.1 mul.163
  103.1 35.2 %custom-call.11 = f32[4,96,96]{2,1,0:T(8,128)S(1)} custom-call(f32[4,96,96]{2,1,0:T(8,128)S(1)} %fusion.9), custom_call_target="Cholesky" | custom-call | tf_op jit(solution)/shard_map/jit(cholesky)/cholesky | solution.py:44
  138.4 0.1 compare_reduce_fusion
  138.6 29.7 %custom-call.12 = f32[4,1,96,96]{2,3,1,0:T(8,128)S(1)} custom-call(f32[4,1,96,96]{3,2,1,0:T(8,128)S(1)} %select_bitcast_fusion), custom_call_target="InvertDiagBlocksLowerTriangular" | custom-call | tf_op jit(solution)/shard_map/vmap(jit(_cho_solve))/triangular_solve | solution.py:47
  168.3 0.8 abs_reduce_fusion.1
  169.4 0.3 convolution_bitcast_fusion
  169.7 0.4 fusion.6
  170.1 0.1 reshape.279
  170.3 8.4 %all_gather.3 = f32[3,32,32]{2,0,1:T(4,128)S(1)} all-gather(f32[3,4,32]{2,0,1:T(4,128)S(1)} %copy.148), channel_id=1, replica_groups=mesh['cells'=8,'wells'=4] {'cells'}, dimensions={1}, use_global_device_ids=true | all-gather | bytes 13824 | tf_op jit(solution)/shard_map/all_gather | solution.py:96
  179.1 0.6 copy.153
  179.8 29.1 %scatter_custom_fusion = f32[3,16384]{0,1:T(8,128)} fusion(s32[4096]{0:T(1024)S(1)} %bitcast.108, f32[4096,3]{1,0:T(8,128)S(1)} %copy.153, f32[]{:T(128)} %constant.69.clone.1), kind=kCustom, calls=%fused_computation.6 | custom fusion | flops 12288 | bytes 196612 | tf_op jit(solution)/shard_map/scatter-add | solution.py:100
  208.9 4.6 %copy.130 = f32[3,1,16384]{0,2,1:T(8,128)} copy(f32[3,1,16384]{2,1,0:T(1,128)S(1)} %copy-done.4) | data formatting | bytes 393216 | tf_op args[1]
  213.5 9.7 %abs_reduce_fusion = (f32[3]{0:T(128)S(1)}, f32[3,16384]{0,1:T(8,128)}) fusion(f32[3,16384]{0,1:T(8,128)} %scatter_custom_fusion, f32[3,1,16384]{0,2,1:T(8,128)} %copy.130), kind=kLoop, calls=%fused_computation.5 | loop fusion | flops 147453 | bytes 589836 | tf_op jit(solution)/shard_map/reduce_max | solution.py:103
  223.2 39.5 %all-reduce.1 = (f32[3]{0:T(128)S(1)}, f32[3]{0:T(128)S(1)}) all-reduce(f32[3]{0:T(128)S(1)} %get-tuple-element.23, f32[3]{0:T(128)S(1)} %get-tuple-element.29), channel_id=1, replica_groups=mesh['cells'=8,'wells'=4] {'cells','wells'}, use_global_device_ids=true, to_apply=%region_11.12 | all-reduce | flops 6 | bytes 48 | tf_op jit(solution)/shard_map/pmax | solution.py:104
  262.7 0.6 pad_maximum_fusion
  263.3 5.4 %copy.154 = f32[3,16384]{1,0:T(4,128)S(1)} copy(f32[3,16384]{0,1:T(8,128)} %get-tuple-element.24) | data formatting | bytes 393216 | tf_op jit(solution)/shard_map/sub | solution.py:102
  268.7 1.4 reduce.6
  270.2 0.3 reshape_squeeze.3
  270.4 0.6 multiply_reduce_fusion
  271.0 0.9 reshape_multiply_fusion
  271.9 0.7 copy.155
  (54 shorter events, 2.1 us)
Async XLA Ops:
  0.6 87.9 %copy-start = (f32[1,32,32]{2,1,0:T(8,128)S(1)}, f32[1,32,32]{2,1,0:T(8,128)}, u32[]{:S(2)}) copy-start(f32[1,32,32]{2,1,0:T(8,128)} %param.19) | copy-start | bytes 12292
  0.6 21.7 %copy-start.5 = (s32[1,32,128]{2,1,0:T(8,128)S(1)}, s32[1,32,128]{2,1,0:T(8,128)}, u32[]{:S(2)}) copy-start(s32[1,32,128]{2,1,0:T(8,128)} %param.15) | copy-start | bytes 49156
  0.7 21.7 %copy-start.8 = (s32[1,32]{1,0:T(1,128)S(1)}, s32[1,32]{1,0:T(1,128)}, u32[]{:S(2)}) copy-start(s32[1,32]{1,0:T(1,128)} %param.16) | copy-start | bytes 388
  0.7 21.7 %copy-start.6 = (f32[1,32,128]{2,1,0:T(8,128)S(1)}, f32[1,32,128]{2,1,0:T(8,128)}, u32[]{:S(2)}) copy-start(f32[1,32,128]{2,1,0:T(8,128)} %param.17) | copy-start | bytes 49156
  0.7 21.8 %copy-start.3 = (f32[3,1,16384]{2,1,0:T(1,128)S(1)}, f32[3,1,16384]{2,1,0:T(1,128)}, u32[]{:S(2)}) copy-start(f32[3,1,16384]{2,1,0:T(1,128)} %param.11) | copy-start | bytes 589828
  7.5 37.1 %copy-start.7 = (f32[3,1,32,32]{3,2,1,0:T(8,128)S(1)}, f32[3,1,32,32]{3,2,1,0:T(8,128)}, u32[]{:S(2)}) copy-start(f32[3,1,32,32]{3,2,1,0:T(8,128)} %param.20) | copy-start | bytes 36868
  27.1 50.3 %copy-start.9 = (u32[32]{0:T(128)S(1)}, u32[32]{0:T(128)}, u32[]{:S(2)}) copy-start(u32[32]{0:T(128)} %constant.96) | copy-start | bytes 388
  101.7 107.1 %copy-start.4 = (f32[3,1,16384]{2,1,0:T(1,128)S(1)}, f32[3,1,16384]{2,1,0:T(1,128)}, u32[]{:S(2)}) copy-start(f32[3,1,16384]{2,1,0:T(1,128)} %param.12) | copy-start | bytes 589828
  213.5 59.1 %copy-start.1 = (f32[1,32,32]{2,1,0:T(8,128)S(1)}, f32[1,32,32]{2,1,0:T(8,128)}, u32[]{:S(2)}) copy-start(f32[1,32,32]{2,1,0:T(8,128)} %param.19) | copy-start | bytes 12292
  223.2 45.5 %copy-start.2 = (f32[9,1,16384]{2,1,0:T(1,128)S(1)}, f32[9,1,16384]{2,1,0:T(1,128)}, u32[]{:S(2)}) copy-start(f32[9,1,16384]{2,1,0:T(1,128)} %param.14) | copy-start | bytes 1769476
where the time goes:
time: 273 us
  other arithmetic  113 us (41%)
  local copies, waits for them, and re-layouts  81.6 us (30%)
  blocking collectives  75.7 us (28%)
    pmax x1, blocking collectives, on_device(): cell_top, well_top = lax.pmax((cell_max, well_max), ('cells', 'wells'))  39.5 us
    another operation x4, other arithmetic, solve_wells(): lower = jnp.linalg.cholesky(dense)  35.4 us
    another operation x3, other arithmetic, one_well(): return jax.scipy.linalg.cho_solve((low, True), vec)  29.8 us
    scatter-add x1, other arithmetic, on_device(): jnp.zeros((3, shard_cells), jnp.float32).at[:, safe.reshape(-1)]  29.1 us
    unnamed x1, blocking collectives  27.8 us
    gather x1, local copies, waits for them, and re-layouts, on_device(): state_at = state[:, safe]  17.5 us
    unnamed x27, local copies, waits for them, and re-layouts  16.8 us
    gather x2, local copies, waits for them, and re-layouts, on_device(): jac_at = cell_block[:, 0][:, safe]  14.8 us

commit v1 on v0

--- a/solution.py
+++ b/solution.py
@@ -2,6 +2,7 @@
 import jax.numpy as jnp
 from jax import lax
 from jax.sharding import PartitionSpec as P
+from jax.lax import all_to_all, axis_size
 
 
 def expand_segments(values, slots):
@@ -93,7 +94,9 @@
     rsum = summed[9:] + source
     solved = solve_wells(ksum, rsum, parent, cond)
     well_max = jnp.max(jnp.abs(rsum), axis=(1, 2))
-    every_well = lax.all_gather(solved, "cells", axis=1, tiled=True)
+    f_now = jnp.stack(tuple((solved for _ in range(axis_size("cells")))))
+    back = all_to_all(f_now, axis_name="cells", concat_axis=0, split_axis=0)
+    every_well = jnp.concatenate(back, axis=1)
     spread = expand_segments(every_well, slots)
     delta = jnp.sum(kmat * spread[None], axis=1)
     correction = (

time: 273 us -> 271 us (level)
  blocking collectives: 75.7 us -> 67.3 us
  starting transfers between devices: 0 us -> 3.34 us
    all_gather x1 -> x0, blocking collectives: 8.42 us -> none  [on_device(): every_well = lax.all_gather(solved, 'cells', axis=1, tiled=True)]
    all_to_all x0 -> x1, starting transfers between devices: none -> 3.34 us  [on_device(): back = all_to_all(f_now, axis_name='cells', concat_axis=0, split_axis=0)]
    unnamed x27 -> x29, local copies, waits for them, and re-layouts: 16.8 us -> 17.6 us
  transfers between devices with their start and end apart: 0 -> 1, of which waited for: 0 -> 0; matrix products, arithmetic and copies ran while one was open for 0% -> 3% of each run, Pallas kernels for 0% -> 0%
where the time goes in v1:
time: 271 us; the launch traced here: 270 us
  other arithmetic  113 us (42%)
  local copies, waits for them, and re-layouts  84.3 us (31%)
  blocking collectives  67.3 us (25%)
  starting transfers between devices  3.34 us (1%)
    pmax x1, blocking collectives, on_device(): cell_top, well_top = lax.pmax((cell_max, well_max), ('cells', 'wells'))  39.5 us
    another operation x4, other arithmetic, solve_wells(): lower = jnp.linalg.cholesky(dense)  35.4 us
    another operation x3, other arithmetic, one_well(): return jax.scipy.linalg.cho_solve((low, True), vec)  29.8 us
    scatter-add x1, other arithmetic, on_device(): jnp.zeros((3, shard_cells), jnp.float32).at[:, safe.reshape(-1)]  29.4 us
    unnamed x1, blocking collectives  27.8 us
    unnamed x29, local copies, waits for them, and re-layouts  17.6 us
    gather x1, local copies, waits for them, and re-layouts, on_device(): state_at = state[:, safe]  17.5 us
    gather x2, local copies, waits for them, and re-layouts, on_device(): jac_at = cell_block[:, 0][:, safe]  14.8 us
  transfers between devices with their start and end apart: 1, of which 0 were waited for; matrix products, arithmetic and copies ran while one was open for 3% of the time, Pallas kernels for 0%

profile of v1, /device:TPU:0, one launch (start us, length us, event | category | flops | bytes accessed | tf_op | source)
XLA Modules:
  0.0 270.5 jit_solution(7044542929450102655)
XLA Ops:
  0.8 6.1 %copy.135 = f32[9,1,16384]{0,2,1:T(8,128)} copy(f32[9,1,16384]{2,1,0:T(1,128)} %param.13) | data formatting | bytes 1179648 | tf_op args[2]
  6.9 14.2 %gather_fusion = f32[4096,9]{1,0:T(8,128)S(1)} fusion(f32[9,16384]{0,1:T(8,128)} %bitcast.92, s32[4096]{0:T(1024)S(1)} %get-tuple-element.27), kind=kCustom, calls=%fused_computation | custom fusion | bytes 311296 | tf_op jit(solution)/shard_map/gather | solution.py:83
  21.0 0.6 copy.136
  21.9 4.6 %copy.142 = f32[3,1,16384]{0,2,1:T(8,128)} copy(f32[3,1,16384]{2,1,0:T(1,128)S(1)} %copy-done.3) | data formatting | bytes 393216 | tf_op args[0]
  26.5 17.5 %gather_fusion.1 = f32[4096,3]{1,0:T(8,128)} fusion(f32[3,16384]{0,1:T(8,128)} %bitcast.93, s32[4096]{0:T(1024)S(1)} %get-tuple-element.27), kind=kCustom, calls=%fused_computation.1 | custom fusion | bytes 114688 | tf_op jit(solution)/shard_map/gather | solution.py:84
  44.0 0.3 copy.143
  44.3 0.4 broadcast_in_dim.77
  44.7 1.9 sub.50
  46.6 0.6 copy.144
  47.2 0.2 copy.139
  47.6 0.1 copy.145
  48.0 0.2 add_multiply_fusion
  48.2 0.6 maximum_reduce_fusion
  48.9 27.8 %all-reduce = f32[12,32,32]{2,1,0:T(8,128)S(1)} all-reduce(f32[12,32,32]{2,1,0:T(8,128)S(1)} %copy.146), channel_id=2, replica_groups=mesh['cells'=8,'wells'=4] {'cells'}, use_global_device_ids=true, to_apply=%region_4.5.clone | all-reduce | flops 12288 | bytes 98304
  76.7 0.6 dynamic-slice.3
  78.0 0.2 copy.147
  78.2 3.1 %mul.160 = f32[4,32,3,32,3]{4,3,2,1,0:T(8,128)} broadcast(f32[4,32,3,3]{3,2,1,0:T(4,128)S(1)} %copy.147), dimensions={0,1,2,4} | broadcast | bytes 152064 | tf_op jit(solution)/shard_map/mul | solution.py:41
  81.2 6.5 %mul.161 = f32[4,96,96]{2,1,0:T(8,128)S(1)} reshape(f32[4,32,3,32,3]{4,3,2,1,0:T(8,128)} %mul.160) | data formatting | bytes 294912 | tf_op jit(solution)/shard_map/mul | solution.py:41
  87.9 0.7 dynamic-slice_bitcast_fusion.1
  88.6 0.6 fusion.5
  89.2 3.5 %mul.150 = f32[4,32,3,32,3]{4,3,2,1,0:T(8,128)} broadcast(f32[4,32,32]{2,1,0:T(8,128)S(1)} %fusion.5), dimensions={0,1,3} | broadcast | bytes 163840 | tf_op jit(solution)/shard_map/mul | solution.py:40
  92.8 6.5 %mul.151 = f32[4,96,96]{2,1,0:T(8,128)S(1)} reshape(f32[4,32,3,32,3]{4,3,2,1,0:T(8,128)} %mul.150) | data formatting | bytes 294912 | tf_op jit(solution)/shard_map/mul | solution.py:40
  99.4 0.2 mul.152
  99.6 1.1 mul.153
  100.8 0.3 mul.162
  101.1 1.1 mul.163
  102.4 35.2 %custom-call.11 = f32[4,96,96]{2,1,0:T(8,128)S(1)} custom-call(f32[4,96,96]{2,1,0:T(8,128)S(1)} %fusion.9), custom_call_target="Cholesky" | custom-call | tf_op jit(solution)/shard_map/jit(cholesky)/cholesky | solution.py:45
  137.9 29.7 %custom-call.12 = f32[4,1,96,96]{2,3,1,0:T(8,128)S(1)} custom-call(f32[4,1,96,96]{3,2,1,0:T(8,128)S(1)} %select_bitcast_fusion), custom_call_target="InvertDiagBlocksLowerTriangular" | custom-call | tf_op jit(solution)/shard_map/vmap(jit(_cho_solve))/triangular_solve | solution.py:48
  167.6 0.8 abs_reduce_fusion.1
  168.7 0.3 convolution_bitcast_fusion
  169.0 0.4 fusion.6
  169.4 0.1 reshape.284
  169.6 0.7 reshape.325
  170.3 3.3 %all-to-all-start = ((f32[8,1,384]{2,1,0:T(1,128)}), f32[8,1,384]{2,1,0:T(1,128)S(1)}, u32[]{:S(2)}, u32[]{:S(2)}) async-start(f32[8,1,384]{2,1,0:T(1,128)} %reshape.325), calls=%async_computation | async-start | bytes 24576 | tf_op jit(solution)/shard_map/all_to_all | solution.py:98
  173.7 4.6 %copy.134 = f32[3,1,16384]{0,2,1:T(8,128)} copy(f32[3,1,16384]{2,1,0:T(1,128)S(1)} %copy-done.4) | data formatting | bytes 393216 | tf_op args[1]
  178.3 1.4 reduce.6
  179.8 0.3 reshape_squeeze.3
  180.0 0.7 copy.160
  180.7 0.5 broadcast.323
  181.2 0.7 reduce.7
  182.4 2.0 copy.158
  184.4 29.4 %scatter_custom_fusion = f32[3,16384]{0,1:T(8,128)} fusion(s32[4096]{0:T(1024)S(1)} %bitcast.112, f32[4096,3]{1,0:T(8,128)} %copy.158, f32[]{:T(128)} %constant.69.clone.1), kind=kCustom, calls=%fused_computation.6 | custom fusion | flops 12288 | bytes 197120 | tf_op jit(solution)/shard_map/scatter-add | solution.py:103
  213.8 9.7 %abs_reduce_fusion = (f32[3]{0:T(128)S(1)}, f32[3,16384]{0,1:T(8,128)}) fusion(f32[3,16384]{0,1:T(8,128)} %scatter_custom_fusion, f32[3,1,16384]{0,2,1:T(8,128)} %copy.134), kind=kLoop, calls=%fused_computation.5 | loop fusion | flops 147453 | bytes 589836 | tf_op jit(solution)/shard_map/reduce_max | solution.py:106
  223.5 39.5 %all-reduce.1 = (f32[3]{0:T(128)S(1)}, f32[3]{0:T(128)S(1)}) all-reduce(f32[3]{0:T(128)S(1)} %get-tuple-element.23, f32[3]{0:T(128)S(1)} %get-tuple-element.29), channel_id=1, replica_groups=mesh['cells'=8,'wells'=4] {'cells','wells'}, use_global_device_ids=true, to_apply=%region_11.12 | all-reduce | flops 6 | bytes 48 | tf_op jit(solution)/shard_map/pmax | solution.py:107
  263.0 0.6 pad_maximum_fusion
  263.6 5.4 %copy.159 = f32[3,16384]{1,0:T(4,128)S(1)} copy(f32[3,16384]{0,1:T(8,128)} %get-tuple-element.24) | data formatting | bytes 393216 | tf_op jit(solution)/shard_map/sub | solution.py:105
  269.0 0.6 multiply_reduce_fusion
  269.6 0.9 reshape_multiply_fusion
  (61 shorter events, 2.4 us)
Async XLA Ops:
  0.6 87.2 %copy-start = (f32[1,32,32]{2,1,0:T(8,128)S(1)}, f32[1,32,32]{2,1,0:T(8,128)}, u32[]{:S(2)}) copy-start(f32[1,32,32]{2,1,0:T(8,128)} %param.19) | copy-start | bytes 12292
  0.6 6.2 %copy-start.5 = (s32[1,32,128]{2,1,0:T(8,128)S(1)}, s32[1,32,128]{2,1,0:T(8,128)}, u32[]{:S(2)}) copy-start(s32[1,32,128]{2,1,0:T(8,128)} %param.15) | copy-start | bytes 49156
  0.7 21.0 %copy-start.6 = (f32[1,32,128]{2,1,0:T(8,128)S(1)}, f32[1,32,128]{2,1,0:T(8,128)}, u32[]{:S(2)}) copy-start(f32[1,32,128]{2,1,0:T(8,128)} %param.17) | copy-start | bytes 49156
  0.7 21.1 %copy-start.8 = (s32[1,32]{1,0:T(1,128)S(1)}, s32[1,32]{1,0:T(1,128)}, u32[]{:S(2)}) copy-start(s32[1,32]{1,0:T(1,128)} %param.16) | copy-start | bytes 388
  0.7 21.2 %copy-start.3 = (f32[3,1,16384]{2,1,0:T(1,128)S(1)}, f32[3,1,16384]{2,1,0:T(1,128)}, u32[]{:S(2)}) copy-start(f32[3,1,16384]{2,1,0:T(1,128)} %param.11) | copy-start | bytes 589828
  6.8 37.2 %copy-start.7 = (f32[3,1,32,32]{3,2,1,0:T(8,128)S(1)}, f32[3,1,32,32]{3,2,1,0:T(8,128)}, u32[]{:S(2)}) copy-start(f32[3,1,32,32]{3,2,1,0:T(8,128)} %param.20) | copy-start | bytes 36868
  26.5 50.2 %copy-start.9 = (u32[32]{0:T(128)S(1)}, u32[32]{0:T(128)}, u32[]{:S(2)}) copy-start(u32[32]{0:T(128)} %constant.96) | copy-start | bytes 388
  92.8 80.9 %copy-start.4 = (f32[3,1,16384]{2,1,0:T(1,128)S(1)}, f32[3,1,16384]{2,1,0:T(1,128)}, u32[]{:S(2)}) copy-start(f32[3,1,16384]{2,1,0:T(1,128)} %param.12) | copy-start | bytes 589828
  99.6 78.7 %copy-start.2 = (f32[9,1,16384]{2,1,0:T(1,128)S(1)}, f32[9,1,16384]{2,1,0:T(1,128)}, u32[]{:S(2)}) copy-start(f32[9,1,16384]{2,1,0:T(1,128)} %param.14) | copy-start | bytes 1769476
  170.3 10.4 %all-to-all-start = ((f32[8,1,384]{2,1,0:T(1,128)}), f32[8,1,384]{2,1,0:T(1,128)S(1)}, u32[]{:S(2)}, u32[]{:S(2)}) async-start(f32[8,1,384]{2,1,0:T(1,128)} %reshape.325), calls=%async_computation | async-start | bytes 24576 | tf_op jit(solution)/shard_map/all_to_all | solution.py:98
  213.8 56.7 %copy-start.1 = (f32[1,32,32]{2,1,0:T(8,128)S(1)}, f32[1,32,32]{2,1,0:T(8,128)}, u32[]{:S(2)}) copy-start(f32[1,32,32]{2,1,0:T(8,128)} %param.19) | copy-start | bytes 12292
